TPU v7x, 32 devices: a whole 2x2x4 slice. The times are simulated.
32 devices in a mesh: dp: 8 (over z, core), tile: 4 (over y, x).
Axes of the slice: x: 2, y: 2, z: 4, core: 2. Of those that a mesh axis runs over, the one named last changes fastest.
Arguments:
- features: bfloat16 [8, 256, 512], P('dp', 'tile'), may hold values from -6 to 6
- depth_probs: float32 [8, 256, 118], P('dp', 'tile'), may hold values from 0 to 1, as said below
- context: bfloat16 [8, 256, 80], P('dp', 'tile'), may hold values from -2 to 2
- bev_grad: bfloat16 [8, 10240, 80], P('dp', 'tile'), may hold values from -18 to 18
- head_weight: bfloat16 [198, 512], replicated, may hold values from -0.4375 to 0.4375
- slot_cell: int32 [8, 4, 4, 512], P('dp', 'tile'), may hold values from 0 to 2559, as said below
- slot_point: int32 [8, 4, 4, 512], P('dp', 'tile'), may hold values from 0 to 7551, as said below
- slot_count: int32 [8, 4, 4], P('dp'), may hold values from 1 to 512, as said below
Outputs:
- grad_features: bfloat16 [8, 256, 512], P('dp', 'tile')
- head_weight_grad: float32 [512, 198], P('tile')
Inputs may be any that keep to these rules, and one draw needn't show every extreme that they name: `slot_count`: every block holds at most 512 live slots; in every scene group one tile receives exactly 512 from every device; the live slots of one device and group sum to at most 7552. `slot_point`: A live slot names a point of the sending device; within one group and sending device each point is named by at most one live slot; dead slots hold 0. `slot_cell`: A live slot names a cell of the receiving tile; dead slots hold 0. `depth_probs`: each pixel's 118 entries are positive and sum to one.
All inputs are finite; a program needn't handle non-finite values.
Results may differ from a plain program's by a relative error of at most 0.0049.
Values may be sent and summed in bfloat16 or wider, within the bound.
A program may use at most 64 MiB of HBM per device.

v0:
```python
import jax
import jax.numpy as jnp
from jax import lax
from jax.sharding import PartitionSpec as P


def lookup(bev_rows, cell_table):
    columns = jnp.arange(bev_rows.shape[0], dtype=jnp.int32)

    def cell_block(block_cells):
        one_hot = (block_cells[:, None] == columns[None, :]).astype(jnp.bfloat16)
        return jnp.dot(one_hot, bev_rows, preferred_element_type=jnp.float32).astype(jnp.bfloat16)

    return lax.map(cell_block, cell_table)


def slot_tables(points, pixels, depth_bins):
    flat_points = points.reshape(-1)
    pixel_of = flat_points // depth_bins
    bin_of = flat_points - pixel_of * depth_bins
    pixel_hot = (pixel_of[:, None] == jnp.arange(pixels, dtype=jnp.int32)[None, :]).astype(
        jnp.bfloat16
    )
    bin_hot = (bin_of[:, None] == jnp.arange(depth_bins, dtype=jnp.int32)[None, :]).astype(
        jnp.float32
    )
    return (pixel_hot, bin_hot)


def slot_probs(pixel_hot, bin_hot, depth_probs):
    spread = jnp.dot(
        pixel_hot.astype(jnp.float32),
        depth_probs,
        precision=lax.Precision.HIGHEST,
        preferred_element_type=jnp.float32,
    )
    return jnp.sum(spread * bin_hot, axis=-1)


def depth_from_slots(pixel_hot, bin_hot, slot_values):
    weighted = bin_hot * slot_values[:, None]
    return jnp.einsum(
        "kp,kd->pd",
        pixel_hot.astype(jnp.float32),
        weighted,
        precision=lax.Precision.HIGHEST,
        preferred_element_type=jnp.float32,
    )


def body(features, depth_probs, context, bev_grad, head_weight, slot_cell, slot_point, slot_count):
    own_index = lax.axis_index("tile")
    features = features[0]
    depth_probs = depth_probs[0]
    context = context[0]
    bev_rows = bev_grad[0]
    cell_table = slot_cell[0, 0]
    points = slot_point[0, 0]
    counts = slot_count[0]
    capacity = cell_table.shape[1]
    pixels, depth_bins = depth_probs.shape
    channels = context.shape[1]
    slot_ids = jnp.arange(capacity, dtype=jnp.int32)
    incoming = lax.dynamic_slice_in_dim(counts, own_index, 1, 1)[:, 0]
    live_in = slot_ids[None, :] < incoming[:, None]
    cell_values = jnp.where(
        live_in[..., None], lookup(bev_rows, cell_table), jnp.zeros((), jnp.bfloat16)
    )
    pixel_hot, bin_hot = slot_tables(points, pixels, depth_bins)
    prob_flat = slot_probs(pixel_hot, bin_hot, depth_probs)
    arrived = lax.all_to_all(cell_values, "tile", split_axis=0, concat_axis=0, tiled=True)
    arrived_flat = arrived.reshape(-1, channels).astype(jnp.float32)
    context_slot = jnp.dot(pixel_hot, context, preferred_element_type=jnp.float32)
    slot_grad = jnp.sum(arrived_flat * context_slot, axis=-1)
    grad_depth = depth_from_slots(pixel_hot, bin_hot, slot_grad)
    grad_ctx = jnp.einsum(
        "kp,kc->pc",
        pixel_hot.astype(jnp.float32),
        prob_flat[:, None] * arrived_flat,
        precision=lax.Precision.HIGHEST,
        preferred_element_type=jnp.float32,
    )
    grad_logits = depth_probs * (
        grad_depth - jnp.sum(depth_probs * grad_depth, axis=-1, keepdims=True)
    )
    head_grad = jnp.concatenate([grad_logits, grad_ctx], axis=-1).astype(jnp.bfloat16)
    grad_feats = jnp.dot(head_grad, head_weight, preferred_element_type=jnp.float32).astype(
        jnp.bfloat16
    )
    weight_share = lax.psum_scatter(
        jnp.dot(features.T, head_grad, preferred_element_type=jnp.float32),
        "tile",
        scatter_dimension=0,
        tiled=True,
    )
    summed = lax.psum(weight_share, "dp")
    return (grad_feats[None], summed)


def solution(mesh):
    return jax.shard_map(
        body,
        mesh=mesh,
        in_specs=(
            P("dp", "tile", None),
            P("dp", "tile", None),
            P("dp", "tile", None),
            P("dp", "tile", None),
            P(),
            P("dp", "tile", None, None),
            P("dp", "tile", None, None),
            P("dp", None, None),
        ),
        out_specs=(P("dp", "tile", None), P("tile", None)),
        check_vma=False,
    )
```

profile of v0, /device:TPU:8, one launch (start us, length us, event | category | flops | bytes accessed | tf_op | source)
XLA Modules:
  0.0 120.5 jit_solution(18162987026569552820)
XLA Ops:
  7.2 1.4 %copy.13 = bf16[1,2560,80]{2,1,0:T(8,128)(2,1)S(1)} copy(bf16[1,2560,80]{1,2,0:T(8,128)(2,1)} %param.13) | data formatting | bytes 819200 | tf_op args[3]
  8.6 7.8 %while.12 = (s32[]{:T(128)}, bf16[4,512,80]{1,2,0:T(8,128)(2,1)S(1)}, s32[4,512]{1,0:T(4,128)}, bf16[2560,80]{1,0:T(8,128)(2,1)S(1)}) while((s32[]{:T(128)}, bf16[4,512,80]{1,2,0:T(8,128)(2,1)S(1)}, s32[4,512]{1,0:T(4,128)}, bf16[2560,80]{1,0:T(8,128)(2,1)S(1)}) %tuple.39), condition=%wide.region_1.2_spmd.clone.clone, body=%wide.region_0.1_spmd.clone.sunk.clone | while | flops 211066880 | bytes 743493 | solution.py:14
  8.6 0.7 constant_dynamic-slice_fusion.3
  9.3 1.2 %fusion.40 = bf16[4,512,80]{1,2,0:T(8,128)(2,1)S(1)} fusion(bf16[4,512,80]{1,2,0:T(8,128)(2,1)S(1)} %get-tuple-element.92, s32[]{:T(128)S(6)} %copy.20, bf16[2560,80]{1,0:T(8,128)(2,1)S(1)} %get-tuple-element.98, s32[512]{0:T(512)S(1)} %bitcast.45), kind=kOutput, calls=%fused_computation.6.clone.1.clone | convolution fusion | flops 211066880 | bytes 739332 | tf_op jit(solution)/shard_map/while/body/eval_jaxpr/dot_general | solution.py:12
  10.5 0.7 constant_dynamic-slice_fusion.3
  11.3 1.2 %fusion.40 = bf16[4,512,80]{1,2,0:T(8,128)(2,1)S(1)} fusion(bf16[4,512,80]{1,2,0:T(8,128)(2,1)S(1)} %get-tuple-element.92, s32[]{:T(128)S(6)} %copy.20, bf16[2560,80]{1,0:T(8,128)(2,1)S(1)} %get-tuple-element.98, s32[512]{0:T(512)S(1)} %bitcast.45), kind=kOutput, calls=%fused_computation.6.clone.1.clone | convolution fusion | flops 211066880 | bytes 739332 | tf_op jit(solution)/shard_map/while/body/eval_jaxpr/dot_general | solution.py:12
  12.5 0.7 constant_dynamic-slice_fusion.3
  13.2 1.2 %fusion.40 = bf16[4,512,80]{1,2,0:T(8,128)(2,1)S(1)} fusion(bf16[4,512,80]{1,2,0:T(8,128)(2,1)S(1)} %get-tuple-element.92, s32[]{:T(128)S(6)} %copy.20, bf16[2560,80]{1,0:T(8,128)(2,1)S(1)} %get-tuple-element.98, s32[512]{0:T(512)S(1)} %bitcast.45), kind=kOutput, calls=%fused_computation.6.clone.1.clone | convolution fusion | flops 211066880 | bytes 739332 | tf_op jit(solution)/shard_map/while/body/eval_jaxpr/dot_general | solution.py:12
  14.5 0.7 constant_dynamic-slice_fusion.3
  15.2 1.2 %fusion.40 = bf16[4,512,80]{1,2,0:T(8,128)(2,1)S(1)} fusion(bf16[4,512,80]{1,2,0:T(8,128)(2,1)S(1)} %get-tuple-element.92, s32[]{:T(128)S(6)} %copy.20, bf16[2560,80]{1,0:T(8,128)(2,1)S(1)} %get-tuple-element.98, s32[512]{0:T(512)S(1)} %bitcast.45), kind=kOutput, calls=%fused_computation.6.clone.1.clone | convolution fusion | flops 211066880 | bytes 739332 | tf_op jit(solution)/shard_map/while/body/eval_jaxpr/dot_general | solution.py:12
  16.4 0.2 dynamic-slice_reduce_fusion
  16.7 0.7 broadcast_select_fusion
  17.4 3.7 %all-to-all-start = ((bf16[4,512,80]{1,2,0:T(8,128)(2,1)}), bf16[4,512,80]{1,2,0:T(8,128)(2,1)S(1)}, u32[]{:S(2)}, u32[]{:S(2)}) async-start(bf16[4,512,80]{1,2,0:T(8,128)(2,1)} %broadcast_select_fusion), calls=%async_computation | async-start | bytes 655360 | tf_op jit(solution)/shard_map/all_to_all | solution.py:71
  21.2 0.9 fusion.7
  22.1 4.9 %all-to-all-done = bf16[4,512,80]{1,2,0:T(8,128)(2,1)S(1)} async-done(((bf16[4,512,80]{1,2,0:T(8,128)(2,1)}), bf16[4,512,80]{1,2,0:T(8,128)(2,1)S(1)}, u32[]{:S(2)}, u32[]{:S(2)}) %all-to-all-start) | async-done | bytes 327712 | tf_op jit(solution)/shard_map/all_to_all | solution.py:71
  27.2 1.1 convolution_convert_fusion.1
  28.3 0.6 fusion.8
  28.8 1.3 %fusion.26 = (f32[64]{0:T(128)S(1)}, f32[64,118]{1,0:T(8,128)S(1)}) fusion(f32[1,64,118]{2,1,0:T(8,128)S(1)} %copy-done.2, f32[2048]{0:T(1024)S(1)} %fusion.8, s32[2048]{0:T(1024)S(1)} %get-tuple-element.48, s32[2048]{0:T(1024)S(1)} %get-tuple-element.49), kind=kOutput, calls=%fused_computation.37 | convolution fusion | flops 186358464 | bytes 85248 | tf_op jit(solution)/shard_map/kp,kd->pd/dot_general | solution.py:42
  30.1 0.1 fusion.27
  30.2 1.0 convolution_bitcast_fusion
  31.3 24.4 %reduce-scatter.2.cloned.1.call-done = f32[128,198]{0,1:T(8,128)} async-done(((f32[512,198]{0,1:T(8,128)}), f32[128,198]{0,1:T(8,128)}) %reduce-scatter.2.cloned.1.call-update) | async-done | bytes 101392 | tf_op jit(solution)/shard_map/reduce_scatter | solution.py:90
  55.7 0.8 fusion.9
  56.6 55.5 %all-reduce.2.cloned.1.call-done = f32[128,198]{0,1:T(8,128)} async-done(((f32[128,198]{0,1:T(8,128)}), f32[128,198]{0,1:T(8,128)}) %all-reduce.2.cloned.1.call-update) | async-done | bytes 101392 | tf_op jit(solution)/shard_map/psum | solution.py:96
  112.1 1.5 %copy.25 = f32[128,198]{0,1:T(8,128)} copy(f32[128,198]{0,1:T(8,128)} %all-reduce.2.cloned.1.call-done) | data formatting | bytes 202752
  (22 shorter events, 0.3 us)
Async XLA Ops:
  7.2 48.5 %copy-start = (bf16[198,512]{1,0:T(8,128)(2,1)S(1)}, bf16[198,512]{1,0:T(8,128)(2,1)}, u32[]{:S(2)}) copy-start(bf16[198,512]{1,0:T(8,128)(2,1)} %param.14) | copy-start | bytes 608260
  8.6 7.9 %copy-start.5 = (s32[1,4,4]{2,1,0:T(4,128)S(1)}, s32[1,4,4]{2,1,0:T(4,128)}, u32[]{:S(2)}) copy-start(s32[1,4,4]{2,1,0:T(4,128)} %param.17) | copy-start | bytes 196
  16.7 4.5 %copy-start.4 = (s32[1,1,4,512]{3,2,1,0:T(4,128)S(1)}, s32[1,1,4,512]{3,2,1,0:T(4,128)}, u32[]{:S(2)}) copy-start(s32[1,1,4,512]{3,2,1,0:T(4,128)} %param.16) | copy-start | bytes 24580
  16.7 4.5 %copy-start.2 = (f32[1,64,118]{2,1,0:T(8,128)S(1)}, f32[1,64,118]{2,1,0:T(8,128)}, u32[]{:S(2)}) copy-start(f32[1,64,118]{2,1,0:T(8,128)} %param.11) | copy-start | bytes 90628
  17.4 9.6 %all-to-all-start = ((bf16[4,512,80]{1,2,0:T(8,128)(2,1)}), bf16[4,512,80]{1,2,0:T(8,128)(2,1)S(1)}, u32[]{:S(2)}, u32[]{:S(2)}) async-start(bf16[4,512,80]{1,2,0:T(8,128)(2,1)} %broadcast_select_fusion), calls=%async_computation | async-start | bytes 655360 | tf_op jit(solution)/shard_map/all_to_all | solution.py:71
  21.2 34.5 %reduce-scatter.2.cloned.1.call-start = ((), (), s32[]{:S(2)}) async-start(), calls=%async_computation.2 | async-start | bytes 512000 | tf_op jit(solution)/shard_map/reduce_scatter | solution.py:90
  27.2 1.1 copy-start.3
  28.8 1.4 %copy-start.1 = (bf16[1,64,512]{2,1,0:T(8,128)(2,1)S(1)}, bf16[1,64,512]{2,1,0:T(8,128)(2,1)}, u32[]{:S(2)}) copy-start(bf16[1,64,512]{2,1,0:T(8,128)(2,1)} %param.10) | copy-start | bytes 196612
  31.3 80.8 %all-reduce.2.cloned.1.call-start = ((), (), s32[]{:S(2)}) async-start(), calls=%async_computation.3 | async-start | bytes 204800 | tf_op jit(solution)/shard_map/psum | solution.py:96
Sparse Core Ops, SparseCore 0:
  31.4 24.2 reduce-scatter.1
  58.0 54.0 all-reduce.1
where the time goes:
time: 121 us; the launch traced here: 120 us
  waiting for transfers between devices  84.8 us (70%)
  between operations  14.2 us (12%)
  matrix products  10.6 us (9%)
  local copies, waits for them, and re-layouts  6.01 us (5%)
  starting transfers between devices  3.76 us (3%)
    psum x1, waiting for transfers between devices, body(): summed = lax.psum(weight_share, 'dp')  55.5 us
    reduce_scatter x1, waiting for transfers between devices, body(): lax.psum_scatter(jnp.dot(features.T, head_grad, preferred_element_type=jn...  24.4 us
    dot_general x4, matrix products, cell_block(): jnp.dot(one_hot, bev_rows, preferred_element_type=jnp.float32)  4.94 us
    all_to_all x1, waiting for transfers between devices, body(): lax.all_to_all(cell_values, 'tile', split_axis=0, concat_axis=0, tiled=True)  4.91 us
    all_to_all x1, starting transfers between devices, body(): lax.all_to_all(cell_values, 'tile', split_axis=0, concat_axis=0, tiled=True)  3.72 us
    unnamed x15, local copies, waits for them, and re-layouts  2.94 us
    dynamic_slice x4, local copies, waits for them, and re-layouts, lookup(): return lax.map(cell_block, cell_table)  2.83 us
  transfers between devices with their start and end apart: 3, of which 3 were waited for; matrix products, arithmetic and copies ran while one was open for 1% of the time, Pallas kernels for 0%

commit v1 on v0

--- a/solution.py
+++ b/solution.py
@@ -93,7 +93,7 @@
         scatter_dimension=0,
         tiled=True,
     )
-    summed = lax.psum(weight_share, "dp")
+    summed = jnp.sum(lax.all_gather(weight_share, "dp"), axis=0)
     return (grad_feats[None], summed)
 
 

time: 121 us -> 82.7 us (0.68)
  the two profiles are of different devices: /device:TPU:8 before, /device:TPU:0 now
where the time goes in v1:
time: 82.7 us; the launch traced here: 82.2 us
  waiting for transfers between devices  28.6 us (35%)
  blocking collectives  15.8 us (19%)
  between operations  14.2 us (17%)
  matrix products  10.6 us (13%)
  local copies, waits for them, and re-layouts  5.95 us (7%)
  starting transfers between devices  5.19 us (6%)
  other arithmetic  1.82 us (2%)
    reduce_scatter x1, waiting for transfers between devices, body(): lax.psum_scatter(jnp.dot(features.T, head_grad, preferred_element_type=jn...  23.7 us
    all_gather x1, blocking collectives, body(): summed = jnp.sum(lax.all_gather(weight_share, 'dp'), axis=0)  15.8 us
    all_to_all x1, starting transfers between devices, body(): lax.all_to_all(cell_values, 'tile', split_axis=0, concat_axis=0, tiled=True)  5.19 us
    dot_general x4, matrix products, cell_block(): jnp.dot(one_hot, bev_rows, preferred_element_type=jnp.float32)  4.93 us
    all_to_all x1, waiting for transfers between devices, body(): lax.all_to_all(cell_values, 'tile', split_axis=0, concat_axis=0, tiled=True)  4.91 us
    dynamic_slice x4, local copies, waits for them, and re-layouts, lookup(): return lax.map(cell_block, cell_table)  2.83 us
    unnamed x13, local copies, waits for them, and re-layouts  2.16 us
  transfers between devices with their start and end apart: 2, of which 2 were waited for; matrix products, arithmetic and copies ran while one was open for 2% of the time, Pallas kernels for 0%

profile of v1, /device:TPU:0, one launch (start us, length us, event | category | flops | bytes accessed | tf_op | source)
XLA Modules:
  0.0 82.2 jit_solution(7944426498755843943)
XLA Ops:
  7.2 0.9 %dynamic-slice_reduce_fusion = s32[4]{0:T(128)S(1)} fusion(s32[1,4,4]{2,1,0:T(4,128)} %param.17, s32[]{:T(128)S(6)} %select_n.20), kind=kLoop, calls=%fused_computation.47 | loop fusion | bytes 36 | tf_op jit(solution)/shard_map/dynamic_slice | solution.py:64
  8.2 1.3 %copy.13 = bf16[1,2560,80]{2,1,0:T(8,128)(2,1)S(1)} copy(bf16[1,2560,80]{1,2,0:T(8,128)(2,1)} %param.13) | data formatting | bytes 819200 | tf_op args[3]
  9.5 7.8 %while.12 = (s32[]{:T(128)}, bf16[4,512,80]{1,2,0:T(8,128)(2,1)S(1)}, s32[4,512]{1,0:T(4,128)}, bf16[2560,80]{1,0:T(8,128)(2,1)S(1)}) while((s32[]{:T(128)}, bf16[4,512,80]{1,2,0:T(8,128)(2,1)S(1)}, s32[4,512]{1,0:T(4,128)}, bf16[2560,80]{1,0:T(8,128)(2,1)S(1)}) %tuple.36), condition=%wide.region_1.2_spmd.clone.clone, body=%wide.region_0.1_spmd.clone.sunk.clone | while | flops 211066880 | bytes 743485 | solution.py:14
  9.5 0.7 constant_dynamic-slice_fusion.3
  10.2 1.2 %fusion.40 = bf16[4,512,80]{1,2,0:T(8,128)(2,1)S(1)} fusion(bf16[4,512,80]{1,2,0:T(8,128)(2,1)S(1)} %get-tuple-element.92, s32[]{:T(128)} %get-tuple-element.91, bf16[2560,80]{1,0:T(8,128)(2,1)S(1)} %get-tuple-element.98, s32[512]{0:T(512)S(1)} %bitcast.53), kind=kOutput, calls=%fused_computation.6.clone.1.clone | convolution fusion | flops 211066880 | bytes 739332 | tf_op jit(solution)/shard_map/while/body/eval_jaxpr/dot_general | solution.py:12
  11.5 0.7 constant_dynamic-slice_fusion.3
  12.2 1.2 %fusion.40 = bf16[4,512,80]{1,2,0:T(8,128)(2,1)S(1)} fusion(bf16[4,512,80]{1,2,0:T(8,128)(2,1)S(1)} %get-tuple-element.92, s32[]{:T(128)} %get-tuple-element.91, bf16[2560,80]{1,0:T(8,128)(2,1)S(1)} %get-tuple-element.98, s32[512]{0:T(512)S(1)} %bitcast.53), kind=kOutput, calls=%fused_computation.6.clone.1.clone | convolution fusion | flops 211066880 | bytes 739332 | tf_op jit(solution)/shard_map/while/body/eval_jaxpr/dot_general | solution.py:12
  13.4 0.7 constant_dynamic-slice_fusion.3
  14.2 1.2 %fusion.40 = bf16[4,512,80]{1,2,0:T(8,128)(2,1)S(1)} fusion(bf16[4,512,80]{1,2,0:T(8,128)(2,1)S(1)} %get-tuple-element.92, s32[]{:T(128)} %get-tuple-element.91, bf16[2560,80]{1,0:T(8,128)(2,1)S(1)} %get-tuple-element.98, s32[512]{0:T(512)S(1)} %bitcast.53), kind=kOutput, calls=%fused_computation.6.clone.1.clone | convolution fusion | flops 211066880 | bytes 739332 | tf_op jit(solution)/shard_map/while/body/eval_jaxpr/dot_general | solution.py:12
  15.4 0.7 constant_dynamic-slice_fusion.3
  16.1 1.2 %fusion.40 = bf16[4,512,80]{1,2,0:T(8,128)(2,1)S(1)} fusion(bf16[4,512,80]{1,2,0:T(8,128)(2,1)S(1)} %get-tuple-element.92, s32[]{:T(128)} %get-tuple-element.91, bf16[2560,80]{1,0:T(8,128)(2,1)S(1)} %get-tuple-element.98, s32[512]{0:T(512)S(1)} %bitcast.53), kind=kOutput, calls=%fused_computation.6.clone.1.clone | convolution fusion | flops 211066880 | bytes 739332 | tf_op jit(solution)/shard_map/while/body/eval_jaxpr/dot_general | solution.py:12
  17.4 0.7 broadcast_select_fusion
  18.1 5.2 %all-to-all-start = ((bf16[4,512,80]{1,2,0:T(8,128)(2,1)}), bf16[4,512,80]{1,2,0:T(8,128)(2,1)S(1)}, u32[]{:S(2)}, u32[]{:S(2)}) async-start(bf16[4,512,80]{1,2,0:T(8,128)(2,1)} %broadcast_select_fusion), calls=%async_computation | async-start | bytes 655360 | tf_op jit(solution)/shard_map/all_to_all | solution.py:71
  23.4 0.9 %fusion.7 = f32[2048]{0:T(1024)S(1)} fusion(s32[2048]{0:T(1024)S(1)} %get-tuple-element.49, s32[2048]{0:T(1024)S(1)} %get-tuple-element.48, f32[1,64,118]{2,1,0:T(8,128)S(1)} %copy-done.2), kind=kOutput, calls=%fused_computation.10 | convolution fusion | flops 186451968 | bytes 54784 | tf_op jit(solution)/shard_map/dot_general | solution.py:31
  24.3 4.9 %all-to-all-done = bf16[4,512,80]{1,2,0:T(8,128)(2,1)S(1)} async-done(((bf16[4,512,80]{1,2,0:T(8,128)(2,1)}), bf16[4,512,80]{1,2,0:T(8,128)(2,1)S(1)}, u32[]{:S(2)}, u32[]{:S(2)}) %all-to-all-start) | async-done | bytes 327712 | tf_op jit(solution)/shard_map/all_to_all | solution.py:71
  29.3 0.7 copy-done.3
  30.0 0.6 fusion.8
  30.6 1.3 %fusion.26 = (f32[64]{0:T(128)S(1)}, f32[64,118]{1,0:T(8,128)S(1)}) fusion(f32[1,64,118]{2,1,0:T(8,128)S(1)} %copy-done.2, f32[2048]{0:T(1024)S(1)} %fusion.8, s32[2048]{0:T(1024)S(1)} %get-tuple-element.48, s32[2048]{0:T(1024)S(1)} %get-tuple-element.49), kind=kOutput, calls=%fused_computation.38 | convolution fusion | flops 186358464 | bytes 85248 | tf_op jit(solution)/shard_map/kp,kd->pd/dot_general | solution.py:42
  31.8 1.1 %convolution_convert_fusion.1 = bf16[64,80]{1,0:T(8,128)(2,1)S(1)} fusion(f32[2048,80]{0,1:T(8,128)S(1)} %bitcast.49, s32[2048]{0:T(1024)S(1)} %get-tuple-element.49, f32[2048]{0:T(1024)S(1)} %fusion.7), kind=kOutput, calls=%fused_computation.15 | convolution fusion | flops 126260224 | bytes 681984 | tf_op jit(solution)/shard_map/kp,kc->pc/dot_general | solution.py:76
  33.0 1.0 %convolution_bitcast_fusion = f32[512,198]{0,1:T(8,128)} fusion(bf16[1,64,512]{2,1,0:T(8,128)(2,1)S(1)} %copy-done.1, bf16[64,80]{1,0:T(8,128)(2,1)S(1)} %convolution_convert_fusion.1, bf16[64,118]{1,0:T(8,128)(2,1)S(1)} %fusion.27), kind=kOutput, calls=%fused_computation.11 | convolution fusion | flops 13026816 | bytes 496384 | tf_op jit(solution)/shard_map/dot_general | solution.py:91
  34.1 0.8 %fusion.9 = bf16[1,64,512]{2,1,0:T(8,128)(2,1)} fusion(bf16[198,512]{1,0:T(8,128)(2,1)S(1)} %copy-done, bf16[64,80]{1,0:T(8,128)(2,1)S(1)} %convolution_convert_fusion.1, bf16[64,118]{1,0:T(8,128)(2,1)S(1)} %fusion.27), kind=kOutput, calls=%fused_computation.14 | convolution fusion | flops 13059584 | bytes 293632 | tf_op jit(solution)/shard_map/dot_general | solution.py:87
  34.9 23.7 %reduce-scatter.2.cloned.1.call-done = f32[128,198]{0,1:T(8,128)} async-done(((f32[512,198]{0,1:T(8,128)}), f32[128,198]{0,1:T(8,128)}) %reduce-scatter.2.cloned.1.call-update) | async-done | bytes 101392 | tf_op jit(solution)/shard_map/reduce_scatter | solution.py:90
  58.6 15.8 %all-gather = f32[1024,198]{0,1:T(8,128)S(1)} all-gather(f32[128,198]{0,1:T(8,128)} %reduce-scatter.2.cloned.1.call-done), channel_id=2, replica_groups=mesh['dp'=8,'tile'=4] {'dp'}, dimensions={0}, use_global_device_ids=true | all-gather | bytes 912384 | tf_op jit(solution)/shard_map/all_gather | solution.py:96
  74.5 0.9 %bitcast_reduce_fusion = f32[128,198]{0,1:T(8,128)} fusion(f32[200,8,128]{2,1,0:T(8,128)S(1)} %bitcast.51), kind=kLoop, calls=%fused_computation.21 | loop fusion | flops 177408 | bytes 912384 | tf_op jit(solution)/shard_map/reduce_sum | solution.py:96
  (19 shorter events, 0.5 us)
Async XLA Ops:
  7.2 26.9 %copy-start = (bf16[198,512]{1,0:T(8,128)(2,1)S(1)}, bf16[198,512]{1,0:T(8,128)(2,1)}, u32[]{:S(2)}) copy-start(bf16[198,512]{1,0:T(8,128)(2,1)} %param.14) | copy-start | bytes 608260
  17.4 6.0 %copy-start.4 = (s32[1,1,4,512]{3,2,1,0:T(4,128)S(1)}, s32[1,1,4,512]{3,2,1,0:T(4,128)}, u32[]{:S(2)}) copy-start(s32[1,1,4,512]{3,2,1,0:T(4,128)} %param.16) | copy-start | bytes 24580
  17.4 6.0 %copy-start.2 = (f32[1,64,118]{2,1,0:T(8,128)S(1)}, f32[1,64,118]{2,1,0:T(8,128)}, u32[]{:S(2)}) copy-start(f32[1,64,118]{2,1,0:T(8,128)} %param.11) | copy-start | bytes 90628
  18.1 11.1 %all-to-all-start = ((bf16[4,512,80]{1,2,0:T(8,128)(2,1)}), bf16[4,512,80]{1,2,0:T(8,128)(2,1)S(1)}, u32[]{:S(2)}, u32[]{:S(2)}) async-start(bf16[4,512,80]{1,2,0:T(8,128)(2,1)} %broadcast_select_fusion), calls=%async_computation | async-start | bytes 655360 | tf_op jit(solution)/shard_map/all_to_all | solution.py:71
  23.3 35.3 %reduce-scatter.2.cloned.1.call-start = ((), (), s32[]{:S(2)}) async-start(), calls=%async_computation.2 | async-start | bytes 512000 | tf_op jit(solution)/shard_map/reduce_scatter | solution.py:90
  29.3 0.7 copy-start.3
  30.6 2.4 %copy-start.1 = (bf16[1,64,512]{2,1,0:T(8,128)(2,1)S(1)}, bf16[1,64,512]{2,1,0:T(8,128)(2,1)}, u32[]{:S(2)}) copy-start(bf16[1,64,512]{2,1,0:T(8,128)(2,1)} %param.10) | copy-start | bytes 196612
Sparse Core Ops, SparseCore 0:
  34.2 24.3 reduce-scatter.1
